TPU v7x, 8 devices: a whole 2x2x1 slice. The times are simulated.
8 devices in a mesh: dp: 2 (over z, y), row: 2 (over x), fsdp: 2 (over core).
Axes of the slice: x: 2, y: 2, z: 1, core: 2. Of those that a mesh axis runs over, the one named last changes fastest.
Arguments:
- x_saved: bfloat16 [2, 24576, 768], P(None, ('dp', 'row', 'fsdp'))
- dy_out: bfloat16 [2, 24576, 768], P(None, ('dp', 'row', 'fsdp'))
- w_gate: bfloat16 [768, 2048], P(None, ('row', 'fsdp'))
- w_up: bfloat16 [768, 2048], P(None, ('row', 'fsdp'))
- w_down: bfloat16 [2048, 768], P(('row', 'fsdp'))
- g_next: float32 [8, 3, 768, 2048], P(('dp', 'row', 'fsdp'))
Outputs:
- output 1: bfloat16 [2, 24576, 768], P(None, ('dp', 'row', 'fsdp'))
- output 2: float32 [3, 768, 2048], P(None, None, ('row', 'fsdp'))
- output 3: float32 [8, 3, 768, 2048], P(('dp', 'row', 'fsdp'))
All inputs are finite; a program needn't handle non-finite values.
Results may differ from a plain program's by a relative error of at most 0.00911145.
Values are sent between devices in bfloat16 or wider.
A program may use at most 1 GiB of HBM per device.

v0:
```python
import jax
import jax.numpy as jnp
from jax import lax
from jax.sharding import PartitionSpec as P

TOK_AXES = ("dp", "row", "fsdp")
GROUP_AXES = ("row", "fsdp")


def mlp_backward(x_flat, dy_flat, w_gate, w_up, w_down):
    pre_gate = jnp.dot(x_flat, w_gate, preferred_element_type=jnp.float32)
    pre_up = jnp.dot(x_flat, w_up, preferred_element_type=jnp.float32)
    sig_gate = jax.nn.sigmoid(pre_gate)
    act_gate = pre_gate * sig_gate
    hidden = (act_gate * pre_up).astype(jnp.bfloat16)
    d_hidden = jnp.einsum("td,fd->tf", dy_flat, w_down, preferred_element_type=jnp.float32)
    d_gate = (d_hidden * pre_up * sig_gate * (1.0 + pre_gate * (1.0 - sig_gate))).astype(jnp.bfloat16)
    d_up = (d_hidden * act_gate).astype(jnp.bfloat16)
    dx_flat = (jnp.einsum("tf,df->td", d_gate, w_gate, preferred_element_type=jnp.float32) + jnp.einsum("tf,df->td", d_up, w_up, preferred_element_type=jnp.float32)).astype(jnp.bfloat16)
    grad_layer = jnp.stack([
        jnp.einsum("td,tf->df", x_flat, d_gate, preferred_element_type=jnp.float32),
        jnp.einsum("td,tf->df", x_flat, d_up, preferred_element_type=jnp.float32),
        jnp.einsum("td,tf->df", dy_flat, hidden, preferred_element_type=jnp.float32),
    ])
    return dx_flat, grad_layer


def solution(mesh):
    def local_step(x_dev, dy_dev, gate_shard, up_shard, down_shard, g_dev):
        w_gate = lax.all_gather(gate_shard, GROUP_AXES, axis=1, tiled=True)
        w_up = lax.all_gather(up_shard, GROUP_AXES, axis=1, tiled=True)
        w_down = lax.all_gather(down_shard, GROUP_AXES, axis=0, tiled=True)
        g_shard = lax.psum_scatter(g_dev[0].astype(jnp.bfloat16), GROUP_AXES, scatter_dimension=2, tiled=True)
        grad_next = lax.psum(g_shard.astype(jnp.float32), "dp")
        micro_count, tok_dev, d_model = x_dev.shape
        dx_flat, grad_layer = mlp_backward(x_dev.reshape(micro_count * tok_dev, d_model), dy_dev.reshape(micro_count * tok_dev, d_model), w_gate, w_up, w_down)
        return dx_flat.reshape(micro_count, tok_dev, d_model), grad_next, grad_layer[None]

    in_specs = (P(None, TOK_AXES, None), P(None, TOK_AXES, None), P(None, GROUP_AXES), P(None, GROUP_AXES), P(GROUP_AXES, None), P(TOK_AXES, None, None, None))
    out_specs = (P(None, TOK_AXES, None), P(None, None, GROUP_AXES), P(TOK_AXES, None, None, None))
    return jax.shard_map(local_step, mesh=mesh, in_specs=in_specs, out_specs=out_specs, check_vma=False)
```

profile of v0, /device:TPU:0, one launch (start us, length us, event | category | flops | bytes accessed | tf_op | source)
XLA Modules:
  0.0 457.8 jit_solution(12924380326927324291)
XLA Ops:
  7.2 0.0 all-gather.6.cloned.1.call-start
  7.2 0.7 all-gather.6.cloned.1.call-update
  7.9 0.0 all-gather.8.cloned.1.call-start
  7.9 0.7 all-gather.8.cloned.1.call-update
  8.6 0.0 all-gather.4.cloned.1.call-start
  8.7 0.7 all-gather.4.cloned.1.call-update
  9.4 0.0 reduce-scatter.2.cloned.1.call-start
  9.4 10.0 %convert_bitcast_fusion = bf16[3,768,2048]{2,1,0:T(8,128)(2,1)} fusion(f32[1,3,768,2048]{3,2,1,0:T(8,128)} %param.11), kind=kLoop, calls=%fused_computation.8 | loop fusion | flops 4718592 | bytes 28311552 | tf_op jit(solution)/shard_map/convert_element_type | solution.py:33
  19.4 0.0 reduce-scatter.2.cloned.1.call-update
  19.5 18.4 %all-gather.6.cloned.1.call-done = bf16[768,2048]{1,0:T(8,128)(2,1)} async-done(((bf16[768,512]{1,0:T(8,128)(2,1)}), bf16[768,2048]{1,0:T(8,128)(2,1)}) %all-gather.6.cloned.1.call-update) | async-done | bytes 3145744 | tf_op jit(solution)/shard_map/all_gather | solution.py:31
  37.8 28.8 %fusion.5 = f32[6144,2048]{1,0:T(8,128)} fusion(bf16[6144,768]{1,0:T(8,128)(2,1)} %bitcast.34, bf16[768,2048]{1,0:T(8,128)(2,1)} %all-gather.6.cloned.1.call-done), kind=kOutput, calls=%fused_computation.13 | convolution fusion | flops 19327352832 | bytes 62914560 | tf_op jit(solution)/shard_map/dot_general | solution.py:12
  66.6 0.0 all-gather.8.cloned.1.call-done
  66.6 29.0 %fusion.6 = f32[6144,2048]{1,0:T(8,128)} fusion(bf16[6144,768]{1,0:T(8,128)(2,1)} %bitcast.35, bf16[768,2048]{1,0:T(8,128)(2,1)} %all-gather.8.cloned.1.call-done), kind=kOutput, calls=%fused_computation.14 | convolution fusion | flops 19327352832 | bytes 62914560 | tf_op jit(solution)/shard_map/dot_general | solution.py:11
  95.6 60.6 %multiply_convert_fusion.1 = (bf16[6144,2048]{1,0:T(8,128)(2,1)}, bf16[6144,2048]{1,0:T(8,128)(2,1)}) fusion(f32[6144,2048]{1,0:T(8,128)} %fusion.6, f32[6144,2048]{1,0:T(8,128)} %fusion.5, bf16[6144,768]{1,0:T(8,128)(2,1)} %bitcast.38, bf16[2048,768]{1,0:T(8,128)(2,1)} %all-gather.4.cloned.1.call-done), kind=kOutput, calls=%fused_computation.1 | convolution fusion | flops 19490930688 | bytes 163577856 | tf_op jit(solution)/shard_map/td,fd->tf/dot_general | solution.py:16
  156.2 29.2 %convolution_bitcast_fusion = f32[1,768,2048]{1,2,0:T(8,128)} fusion(bf16[6144,2048]{1,0:T(8,128)(2,1)} %get-tuple-element.6, bf16[6144,768]{1,0:T(8,128)(2,1)} %bitcast.36), kind=kOutput, calls=%fused_computation.10 | convolution fusion | flops 19327352832 | bytes 40894464 | tf_op jit(solution)/shard_map/td,tf->df/dot_general | solution.py:22
  185.4 0.0 copy-done
  185.4 24.4 %convolution_bitcast_fusion.1 = f32[1,768,2048]{1,2,0:T(8,128)} fusion(bf16[6144,2048]{1,0:T(8,128)(2,1)} %get-tuple-element.7, bf16[6144,768]{1,0:T(8,128)(2,1)S(1)} %bitcast.37), kind=kOutput, calls=%fused_computation.11 | convolution fusion | flops 19327352832 | bytes 40894464 | tf_op jit(solution)/shard_map/td,tf->df/dot_general | solution.py:21
  209.7 40.9 %fusion.3 = f32[1,768,2048]{1,2,0:T(8,128)} fusion(bf16[6144,768]{1,0:T(8,128)(2,1)} %bitcast.39, f32[6144,2048]{1,0:T(8,128)} %fusion.5, f32[6144,2048]{1,0:T(8,128)} %fusion.6), kind=kOutput, calls=%fused_computation.9 | convolution fusion | flops 19402850304 | bytes 116391936 | tf_op jit(solution)/shard_map/td,tf->df/dot_general | solution.py:23
  250.6 14.6 %maximum_bitcast_fusion = f32[1,3,768,2048]{2,3,1,0:T(8,128)} fusion(f32[1,768,2048]{1,2,0:T(8,128)} %fusion.3, f32[1,768,2048]{1,2,0:T(8,128)} %convolution_bitcast_fusion, f32[1,768,2048]{1,2,0:T(8,128)} %convolution_bitcast_fusion.1), kind=kLoop, calls=%fused_computation.6 | loop fusion | flops 9437184 | bytes 37748736 | tf_op jit(solution)/shard_map/broadcast_in_dim | solution.py:37
  265.2 18.7 %copy.9 = f32[1,3,768,2048]{3,2,1,0:T(8,128)} copy(f32[1,3,768,2048]{2,3,1,0:T(8,128)} %maximum_bitcast_fusion) | data formatting | bytes 37748736
  283.9 26.5 %fusion.7 = f32[6144,768]{1,0:T(8,128)} fusion(bf16[6144,2048]{1,0:T(8,128)(2,1)} %get-tuple-element.7, bf16[768,2048]{1,0:T(8,128)(2,1)} %all-gather.8.cloned.1.call-done), kind=kOutput, calls=%fused_computation.15 | convolution fusion | flops 19327352832 | bytes 47185920 | tf_op jit(solution)/shard_map/tf,df->td/dot_general | solution.py:19
  310.3 0.0 copy-done.1
  310.3 27.5 %add_convert_fusion = bf16[6144,768]{1,0:T(8,128)(2,1)} fusion(f32[6144,768]{1,0:T(8,128)} %fusion.7, bf16[6144,2048]{1,0:T(8,128)(2,1)} %get-tuple-element.6, bf16[768,2048]{1,0:T(8,128)(2,1)S(1)} %copy-done.1), kind=kOutput, calls=%fused_computation.7 | convolution fusion | flops 19336790016 | bytes 56623104 | tf_op jit(solution)/shard_map/tf,df->td/dot_general | solution.py:19
  337.9 113.2 %all-reduce.1 = f32[3,768,512]{2,1,0:T(8,128)} all-reduce(bf16[3,768,512]{2,1,0:T(8,128)(2,1)} %reduce-scatter.2.cloned.1.call-done), channel_id=1, replica_groups=mesh['dp'=2,'row'=2,'fsdp'=2] {'dp'}, use_global_device_ids=true, to_apply=%region_1.0 | all-reduce | flops 1179648 | bytes 7077888 | tf_op jit(solution)/shard_map/psum | solution.py:34
  (4 shorter events, 0.0 us)
Async XLA Ops:
  7.2 30.6 %all-gather.6.cloned.1.call-start = ((), (), s32[]{:S(2)}) async-start(), calls=%async_computation.2 | async-start | bytes 3932160 | tf_op jit(solution)/shard_map/all_gather | solution.py:31
  7.9 58.7 %all-gather.8.cloned.1.call-start = ((), (), s32[]{:S(2)}) async-start(), calls=%async_computation.3 | async-start | bytes 3932160 | tf_op jit(solution)/shard_map/all_gather | solution.py:30
  8.6 87.0 %all-gather.4.cloned.1.call-start = ((), (), s32[]{:S(2)}) async-start(), calls=%async_computation.1 | async-start | bytes 3932160 | tf_op jit(solution)/shard_map/all_gather | solution.py:32
  9.4 328.5 %reduce-scatter.2.cloned.1.call-start = ((), (), s32[]{:S(2)}) async-start(), calls=%async_computation.4 | async-start | bytes 11796480 | tf_op jit(solution)/shard_map/reduce_scatter | solution.py:33
  156.2 29.2 %copy-start = (bf16[2,3072,768]{2,1,0:T(8,128)(2,1)S(1)}, bf16[2,3072,768]{2,1,0:T(8,128)(2,1)}, u32[]{:S(2)}) copy-start(bf16[2,3072,768]{2,1,0:T(8,128)(2,1)} %param.6) | copy-start | bytes 28311556
  283.9 26.5 %copy-start.1 = (bf16[768,2048]{1,0:T(8,128)(2,1)S(1)}, bf16[768,2048]{1,0:T(8,128)(2,1)}, u32[]{:S(2)}) copy-start(bf16[768,2048]{1,0:T(8,128)(2,1)} %all-gather.6.cloned.1.call-done) | copy-start | bytes 9437188
Sparse Core Ops, SparseCore 0:
  9.5 28.2 all-gather.5
  39.3 25.4 all-gather.7
  66.4 25.4 all-gather.3
  94.2 71.5 reduce-scatter.1
where the time goes:
time: 463 us; the launch traced here: 458 us
  matrix products  267 us (58%)
  blocking collectives  113 us (24%)
  other arithmetic  24.6 us (5%)
  waiting for transfers between devices  20.4 us (4%)
  local copies, waits for them, and re-layouts  18.7 us (4%)
  between operations  14 us (3%)
    psum x1, blocking collectives, local_step(): grad_next = lax.psum(g_shard.astype(jnp.float32), 'dp')  113 us
    dot_general x1, matrix products, mlp_backward(): jnp.einsum('td,fd->tf', dy_flat, w_down, preferred_element_type=jnp.float32)  60.6 us
    dot_general x1, matrix products, mlp_backward(): jnp.einsum('td,tf->df', dy_flat, hidden, preferred_element_type=jnp.float32)  40.9 us
    dot_general x1, matrix products, mlp_backward(): jnp.einsum('td,tf->df', x_flat, d_up, preferred_element_type=jnp.float32)  29.2 us
    dot_general x1, matrix products, mlp_backward(): pre_gate = jnp.dot(x_flat, w_gate, preferred_element_type=jnp.float32)  29 us
    dot_general x1, matrix products, mlp_backward(): pre_up = jnp.dot(x_flat, w_up, preferred_element_type=jnp.float32)  28.8 us
    dot_general x1, matrix products, mlp_backward(): jnp.einsum('tf,df->td', d_up, w_up, preferred_element_type=jnp.float32)  27.5 us
    dot_general x1, matrix products, mlp_backward(): jnp.einsum('tf,df->td', d_gate, w_gate, preferred_element_type=jnp.float32)  26.5 us
  transfers between devices with their start and end apart: 4, of which 1 were waited for; matrix products, arithmetic and copies ran while one was open for 68% of the time, Pallas kernels for 0%

commit v1 on v0

v1 whole, which is shorter than its diff:
```python
import functools

import jax
import jax.numpy as jnp
from jax import lax
from jax.experimental import pallas as pl
from jax.experimental.pallas import tpu as pltpu
from jax.sharding import PartitionSpec as P

TOK_AXES = ("dp", "row", "fsdp")
GROUP_AXES = ("row", "fsdp")
VMEM_BYTES = 67_000_000
MESH = pl.DeviceIdType.MESH

TILE1 = 768
TILE2 = 1024
SHARDS1 = 3
CHUNKS = 16
CORE_SUM = 3
ROW_SUM = 13
FORWARD = 12


def dot(lhs, rhs, lhs_dim, rhs_dim):
    return lax.dot_general(lhs, rhs, (((lhs_dim,), (rhs_dim,)), ((), ())), preferred_element_type=jnp.float32)


def wide_sum(a, b):
    return (a.astype(jnp.float32) + b.astype(jnp.float32)).astype(jnp.bfloat16)


def backward_tile(x_ref, dy_ref, w13, w2, z_ref, h_ref, dw_ref, first, rows, put_dx):
    tile, ff = h_ref.shape
    for r in range(tile // rows):
        sl = slice(r * rows, (r + 1) * rows)
        ab = dot(x_ref[sl, :], w13[...], 1, 0)
        dh = dot(dy_ref[sl, :], w2[...], 1, 1)
        gate, up = ab[:, :ff], ab[:, ff:]
        sig = jax.nn.sigmoid(gate)
        act = gate * sig
        h_ref[sl, :] = (act * up).astype(jnp.bfloat16)
        z_ref[sl, :ff] = (dh * up * (sig + act * (1.0 - sig))).astype(jnp.bfloat16)
        z_ref[sl, ff:] = (dh * act).astype(jnp.bfloat16)
        put_dx(r, dot(z_ref[sl, :], w13[...], 1, 1))
    dw13 = dot(x_ref[...], z_ref[...], 0, 0)
    terms = (dw13[:, :ff], dw13[:, ff:], dot(dy_ref[...], h_ref[...], 0, 0))
    for slab, term in enumerate(terms):
        dw_ref[slab] = jnp.where(first, 0.0, dw_ref[slab]) + term


def first_kernel(
    x_ref, dy_ref, g_ref, w1_ref, w3_ref, w2_ref,
    dxp_ref, dws_ref, f1_ref, f3_ref, f2_ref, r_ref, c_ref,
    acc_ref, w13s_ref, w2s_ref, z_ref, h_ref, send_ref, own_ref, core_ref, row_ref,
    w_loc, w_core, w_row, w_fwd, a_sem, b_sem, c_sem, out_sem, dx_sem,
):
    shard, tile = pl.program_id(0), pl.program_id(1)
    tiles = pl.num_programs(1)
    step = shard * tiles + tile
    steps = SHARDS1 * tiles
    dp, row, core = (lax.axis_index(a) for a in TOK_AXES)
    mate = (dp, row, 1 - core)
    across = (dp, 1 - row, core)
    replica = (1 - dp, row, core)
    ff = h_ref.shape[1]
    chunk = g_ref.shape[0]

    def push(src, dst, sems, k, to):
        return pltpu.make_async_remote_copy(
            src_ref=src, dst_ref=dst, send_sem=sems.at[0, k], recv_sem=sems.at[1, k], device_id=to, device_id_type=MESH
        )

    def slots(s):
        return w13s_ref.at[s, :, :ff], w13s_ref.at[s, :, ff:], w2s_ref.at[s]

    weights = (w1_ref, w3_ref, w2_ref)
    local = [pltpu.make_async_copy(w, d, w_loc.at[k]) for k, (w, d) in enumerate(zip(weights, slots(0)))]
    to_mate = [push(w, d, w_core, k, mate) for k, (w, d) in enumerate(zip(weights, slots(1)))]
    to_row = [push(w, d, w_row, k, across) for k, (w, d) in enumerate(zip(weights, slots(2)))]
    forward = [push(w, d, w_fwd, k, mate) for k, (w, d) in enumerate(zip(slots(2), (f1_ref, f3_ref, f2_ref)))]

    def rows_of(c):
        return pl.ds(pl.multiple_of(c * chunk, 16), chunk)

    def core_push(c):
        return push(send_ref.at[lax.rem(c, 2)], core_ref.at[:, rows_of(c), :], a_sem, c, mate)

    def row_push(c):
        return push(own_ref.at[1, rows_of(c), :], row_ref.at[rows_of(c), :], b_sem, c, across)

    def dp_push(c):
        return push(own_ref.at[0, rows_of(c), :], c_ref.at[rows_of(c), :], c_sem, c, replica)

    keep_sum = pltpu.make_async_copy(own_ref.at[0], r_ref, out_sem)

    def dx_rows(t):
        return pl.ds(pl.multiple_of(t * TILE1, TILE1), TILE1)

    def dx_out(t):
        return pltpu.make_async_copy(acc_ref.at[dx_rows(t), :], dxp_ref.at[dx_rows(t), :], dx_sem.at[t])

    @pl.when(step == 0)
    def _():
        barrier = pltpu.get_barrier_semaphore()
        for to in (mate, across, replica):
            pl.semaphore_signal(barrier, inc=1, device_id=to, device_id_type=MESH)
        for copy in local:
            copy.start()
        pl.semaphore_wait(barrier, 3)
        for copy in (*to_row, *to_mate):
            copy.start()
        for copy in local:
            copy.wait()

    @pl.when(step == tiles)
    def _():
        for copy in to_mate:
            copy.wait_recv()

    @pl.when(step == FORWARD)
    def _():
        for copy in to_row:
            copy.wait_recv()
        for copy in forward:
            copy.start()

    @pl.when((step >= 1) & (step <= CHUNKS))
    def _():
        core_push(step - 1).start()

    @pl.when(step < CHUNKS)
    def _():
        @pl.when(step >= 2)
        def _():
            core_push(step - 2).wait_send()

        for k, r in enumerate((row, 1 - row)):
            mine = pl.ds(pl.multiple_of((2 * r + core) * ff, ff), ff)
            theirs = pl.ds(pl.multiple_of((2 * r + 1 - core) * ff, ff), ff)
            own_ref[k, rows_of(step), :] = g_ref[:, mine].astype(jnp.bfloat16)
            send_ref[lax.rem(step, 2), k] = g_ref[:, theirs].astype(jnp.bfloat16)

    @pl.when((step > CORE_SUM) & (step <= CORE_SUM + CHUNKS))
    def _():
        row_push(step - CORE_SUM - 1).start()

    @pl.when((step >= CORE_SUM) & (step < CORE_SUM + CHUNKS))
    def _():
        c = step - CORE_SUM
        core_push(c).wait_recv()
        for k in range(2):
            own_ref[k, rows_of(c), :] = wide_sum(own_ref[k, rows_of(c), :], core_ref[k, rows_of(c), :])

    @pl.when((step > ROW_SUM) & (step <= ROW_SUM + CHUNKS // 2))
    def _():
        for k in range(2):
            dp_push(2 * (step - ROW_SUM - 1) + k).start()

    @pl.when((step >= ROW_SUM) & (step < ROW_SUM + CHUNKS // 2))
    def _():
        for k in range(2):
            c = 2 * (step - ROW_SUM) + k
            row_push(c).wait_recv()
            own_ref[0, rows_of(c), :] = wide_sum(own_ref[0, rows_of(c), :], row_ref[rows_of(c), :])

    @pl.when(step == ROW_SUM + CHUNKS // 2 + 1)
    def _():
        keep_sum.start()

    @pl.when(step > steps - tiles)
    def _():
        dx_out(tile - 1).start()

    rows = TILE1 // 2

    def put_dx(r, dx):
        sl = pl.ds(pl.multiple_of(tile * TILE1 + r * rows, rows), rows)
        acc_ref[sl, :] = jnp.where(shard == 0, 0.0, acc_ref[sl, :]) + dx

    backward_tile(x_ref, dy_ref, w13s_ref.at[shard], w2s_ref.at[shard], z_ref, h_ref, dws_ref.at[0], tile == 0, rows, put_dx)

    @pl.when(step == steps - 1)
    def _():
        dx_out(tile).start()
        for copy in (*to_mate, *to_row):
            copy.wait_send()
        for copy in forward:
            copy.wait()
        core_push(CHUNKS - 2).wait_send()
        core_push(CHUNKS - 1).wait_send()
        for c in range(CHUNKS):
            row_push(c).wait_send()
            dp_push(c).wait()
        keep_sum.wait()
        for t in range(dxp_ref.shape[0] // TILE1):
            dx_out(t).wait()


def run_first(x, dy, weights, g):
    tokens, d = x.shape
    ff = weights[0].shape[1]
    g_rows, g_cols = g.shape
    chunk = g_rows // CHUNKS
    tiles = tokens // TILE1
    hbm = pl.BlockSpec(memory_space=pltpu.HBM)
    tok = pl.BlockSpec((TILE1, d), lambda s, j: (j, 0))
    bf16, f32, dma = jnp.bfloat16, jnp.float32, pltpu.SemaphoreType.DMA
    like = lambda v: jax.ShapeDtypeStruct(v.shape, v.dtype)
    return pl.pallas_call(
        first_kernel,
        grid=(SHARDS1, tiles),
        in_specs=[tok, tok, pl.BlockSpec((chunk, g_cols), lambda s, j: (jnp.minimum(s * tiles + j, CHUNKS - 1), 0)), hbm, hbm, hbm],
        out_specs=[hbm, pl.BlockSpec((1, 3, d, ff), lambda s, j: (s, 0, 0, 0)), hbm, hbm, hbm, hbm, hbm],
        out_shape=[
            jax.ShapeDtypeStruct((tokens, d), f32),
            jax.ShapeDtypeStruct((SHARDS1, 3, d, ff), f32),
            *[like(w) for w in weights],
            jax.ShapeDtypeStruct((g_rows, ff), bf16),
            jax.ShapeDtypeStruct((g_rows, ff), bf16),
        ],
        scratch_shapes=[
            pltpu.VMEM((tokens, d), f32),
            pltpu.VMEM((SHARDS1, d, 2 * ff), bf16),
            pltpu.VMEM((SHARDS1, ff, d), bf16),
            pltpu.VMEM((TILE1, 2 * ff), bf16),
            pltpu.VMEM((TILE1, ff), bf16),
            pltpu.VMEM((2, 2, chunk, ff), bf16),
            pltpu.VMEM((2, g_rows, ff), bf16),
            pltpu.VMEM((2, g_rows, ff), bf16),
            pltpu.VMEM((g_rows, ff), bf16),
            dma((3,)),
            dma((2, 3)),
            dma((2, 3)),
            dma((2, 3)),
            dma((2, CHUNKS)),
            dma((2, CHUNKS)),
            dma((2, CHUNKS)),
            dma(()),
            dma((tiles,)),
        ],
        compiler_params=pltpu.CompilerParams(
            vmem_limit_bytes=VMEM_BYTES, dimension_semantics=("arbitrary", "arbitrary"), collective_id=0, has_side_effects=True
        ),
        cost_estimate=pl.CostEstimate(flops=16 * SHARDS1 * tokens * d * ff, bytes_accessed=120_000_000, transcendentals=0),
        name="bwd_first",
    )(x, dy, g, *weights)


def last_kernel(
    x_ref, dy_ref, dxp_ref, dws_ref, w1_ref, w3_ref, w2_ref, r_ref, c_ref,
    dx_ref, next_ref, dw_ref,
    w13s_ref, z_ref, h_ref, dw_acc, move_sem, own_sem,
):
    tile, tiles = pl.program_id(0), pl.num_programs(0)
    row, core = lax.axis_index("row"), lax.axis_index("fsdp")
    ff = h_ref.shape[1]
    block = dws_ref.shape[2]
    cols = [2 * row + core, 2 * row + 1 - core, 2 * (1 - row) + core, 2 * (1 - row) + 1 - core]
    lanes = [pl.ds(pl.multiple_of(q * ff, ff), ff) for q in cols]
    span = pl.ds(pl.multiple_of(tile * block, block), block)
    moves = [pltpu.make_async_copy(dws_ref.at[s], dw_ref.at[:, span, lanes[s]], move_sem.at[s]) for s in range(SHARDS1)]
    for move in moves:
        move.start()

    @pl.when(tile == 0)
    def _():
        w13s_ref[:, :ff] = w1_ref[...]
        w13s_ref[:, ff:] = w3_ref[...]

    next_ref[...] = r_ref[...].astype(jnp.float32) + c_ref[...].astype(jnp.float32)
    rows = TILE2 // 2

    def put_dx(r, dx):
        sl = slice(r * rows, (r + 1) * rows)
        dx_ref[sl, :] = (dxp_ref[sl, :] + dx).astype(jnp.bfloat16)

    backward_tile(x_ref, dy_ref, w13s_ref, w2_ref, z_ref, h_ref, dw_acc, tile == 0, rows, put_dx)
    for move in moves:
        move.wait()

    @pl.when(tile == tiles - 1)
    def _():
        own = pltpu.make_async_copy(dw_acc, dw_ref.at[:, :, lanes[3]], own_sem)
        own.start()
        own.wait()


def run_last(x, dy, dxp, dws, weights, mine, other):
    tokens, d = x.shape
    ff = weights[0].shape[1]
    tiles = tokens // TILE2
    g_rows = mine.shape[0]
    tok = pl.BlockSpec((TILE2, d), lambda j: (j, 0))
    full = lambda w: pl.BlockSpec(w.shape, lambda j: (0, 0))
    part = pl.BlockSpec((g_rows // tiles, ff), lambda j: (j, 0))
    return pl.pallas_call(
        last_kernel,
        grid=(tiles,),
        in_specs=[tok, tok, tok, pl.BlockSpec((SHARDS1, 3, d // tiles, ff), lambda j: (0, 0, j, 0)), *[full(w) for w in weights], part, part],
        out_specs=[tok, part, pl.BlockSpec(memory_space=pltpu.HBM)],
        out_shape=[
            jax.ShapeDtypeStruct((tokens, d), jnp.bfloat16),
            jax.ShapeDtypeStruct((g_rows, ff), jnp.float32),
            jax.ShapeDtypeStruct((3, d, 4 * ff), jnp.float32),
        ],
        scratch_shapes=[
            pltpu.VMEM((d, 2 * ff), jnp.bfloat16),
            pltpu.VMEM((TILE2, 2 * ff), jnp.bfloat16),
            pltpu.VMEM((TILE2, ff), jnp.bfloat16),
            pltpu.VMEM((3, d, ff), jnp.float32),
            pltpu.SemaphoreType.DMA((SHARDS1,)),
            pltpu.SemaphoreType.DMA(()),
        ],
        compiler_params=pltpu.CompilerParams(vmem_limit_bytes=VMEM_BYTES, dimension_semantics=("arbitrary",)),
        cost_estimate=pl.CostEstimate(flops=16 * tokens * d * ff, bytes_accessed=90_000_000, transcendentals=0),
        name="bwd_last",
    )(x, dy, dxp, dws, *weights, mine, other)


def solution(mesh):
    def local_step(x_dev, dy_dev, gate_shard, up_shard, down_shard, g_dev):
        micro_count, tok_dev, d_model = x_dev.shape
        ff = gate_shard.shape[1]
        x, dy = (v.reshape(micro_count * tok_dev, d_model) for v in (x_dev, dy_dev))
        g = g_dev.reshape(3 * d_model, 4 * ff)
        dxp, dws, *far, mine, other = run_first(x, dy, (gate_shard, up_shard, down_shard), g)
        dx, grad_next, grad_layer = run_last(x, dy, dxp, dws, far, mine, other)
        return dx.reshape(micro_count, tok_dev, d_model), grad_next.reshape(3, d_model, ff), grad_layer[None]

    in_specs = (P(None, TOK_AXES, None), P(None, TOK_AXES, None), P(None, GROUP_AXES), P(None, GROUP_AXES), P(GROUP_AXES, None), P(TOK_AXES, None, None, None))
    out_specs = (P(None, TOK_AXES, None), P(None, None, GROUP_AXES), P(TOK_AXES, None, None, None))
    return jax.shard_map(local_step, mesh=mesh, in_specs=in_specs, out_specs=out_specs, check_vma=False)
```

time: 463 us -> 202 us (0.44); the launches traced: 458 us -> 201 us
  matrix products: 267 us -> 0 us
  Pallas kernels: 0 us -> 201 us
  blocking collectives: 113 us -> 0 us
  other arithmetic: 24.6 us -> 0 us
  waiting for transfers between devices: 20.4 us -> 0 us
  local copies, waits for them, and re-layouts: 18.7 us -> 0 us
  between operations: 14 us -> 0.64 us
    dot_general x8 -> x0, matrix products: 267 us -> none  [the longest x1 60.6 us: mlp_backward(): jnp.einsum('td,fd->tf', dy_flat, w_down, preferred_element_type=jnp.float32)]
    pallas_call x0 -> x2, Pallas kernels: none -> 201 us  [the longest x1 148 us: run_first(): pl.pallas_call(first_kernel, grid=(SHARDS1, tiles), in_specs=[tok, tok, p...]
    psum x1 -> x0, blocking collectives: 113 us -> none  [local_step(): grad_next = lax.psum(g_shard.astype(jnp.float32), 'dp')]
    unnamed x5 -> x0, local copies, waits for them, and re-layouts: 18.7 us -> none
    all_gather x3 -> x0, waiting for transfers between devices: 18.4 us -> none  [the longest x1 18.4 us: local_step(): w_up = lax.all_gather(up_shard, GROUP_AXES, axis=1, tiled=True)]
    broadcast_in_dim x1 -> x0, other arithmetic: 14.6 us -> none  [local_step(): grad_layer[None]]
    convert_element_type x1 -> x0, other arithmetic: 10 us -> none  [local_step(): g_dev[0].astype(jnp.bfloat16)]
  transfers between devices with their start and end apart: 4 -> 0, of which waited for: 1 -> 0; matrix products, arithmetic and copies ran while one was open for 68% -> 0% of each run, Pallas kernels for 0% -> 0%
where the time goes in v1:
time: 202 us; the launch traced here: 201 us
  Pallas kernels  201 us (100%)
    pallas_call x1, Pallas kernels, run_first(): pl.pallas_call(first_kernel, grid=(SHARDS1, tiles), in_specs=[tok, tok, p...  148 us
    pallas_call x1, Pallas kernels, run_last(): pl.pallas_call(last_kernel, grid=(tiles,), in_specs=[tok, tok, tok, pl.Bl...  52.9 us

profile of v1, /device:TPU:0, one launch (start us, length us, event | category | flops | bytes accessed | tf_op | source)
XLA Modules:
  0.0 201.5 jit_solution(3124203965740956542)
XLA Ops:
  0.6 148.0 %bwd_first.1 = (f32[6144,768]{1,0:T(8,128)}, f32[3,3,768,512]{3,2,1,0:T(8,128)}, bf16[768,512]{1,0:T(8,128)(2,1)}, bf16[768,512]{1,0:T(8,128)(2,1)}, bf16[512,76...) custom-call(bf16[6144,768]{1,0:T(8,128)(2,1)} %bitcast.7, bf16[6144,768]{1,0:T(8,128)(2,1)} %bitcast.9, ...), custom_call_target="tpu_custom_call" | custom-call | flops 115964116992 | bytes 120000000 | tf_op jit(solution)/shard_map/bwd_first/pallas_call | solution.py:209
  148.6 52.9 %bwd_last.1 = (bf16[6144,768]{1,0:T(8,128)(2,1)}, f32[2304,512]{1,0:T(8,128)}, f32[3,768,2048]{2,1,0:T(8,128)}) custom-call(bf16[6144,768]{1,0:T(8,128)(2,1)} %bitcast.8, bf16[6144,768]{1,0:T(8,128)(2,1)} %bitcast.10, f32[6144,768]{1,0:T(8,128)} %get-tuple-element.13.dxp_ref, f32[3,3,768,512]{3,2,1,0:T(8,128)} %get-tuple-element.14.dws_ref, ...), custom_call_target="tpu_custom_call" | custom-call | flops 38654705664 | bytes 90000000 | tf_op jit(solution)/shard_map/bwd_last/pallas_call | solution.py:296

commit v2 on v1

--- a/solution.py
+++ b/solution.py
@@ -13,11 +13,13 @@
 MESH = pl.DeviceIdType.MESH
 
 TILE1 = 768
-TILE2 = 1024
+TILE2 = 768
+COLS = 256
+MOVE = 128
 SHARDS1 = 3
 CHUNKS = 16
 CORE_SUM = 3
-ROW_SUM = 13
+ROW_SUM = 14
 FORWARD = 12
 
 
@@ -29,29 +31,34 @@
     return (a.astype(jnp.float32) + b.astype(jnp.float32)).astype(jnp.bfloat16)
 
 
-def backward_tile(x_ref, dy_ref, w13, w2, z_ref, h_ref, dw_ref, first, rows, put_dx):
-    tile, ff = h_ref.shape
-    for r in range(tile // rows):
-        sl = slice(r * rows, (r + 1) * rows)
-        ab = dot(x_ref[sl, :], w13[...], 1, 0)
-        dh = dot(dy_ref[sl, :], w2[...], 1, 1)
-        gate, up = ab[:, :ff], ab[:, ff:]
+def by_rows(rows, block, body):
+    @pl.loop(0, rows // block)
+    def _(i):
+        body(pl.ds(pl.multiple_of(i * block, block), block))
+
+
+def backward_tile(x_ref, dy_ref, w13_ref, w2_ref, z_ref, h_ref, dw_ref, first, put_dx):
+    ff = h_ref.shape[1]
+    for c in range(0, ff, COLS):
+        gate = dot(x_ref[...], w13_ref[:, c : c + COLS], 1, 0)
+        up = dot(x_ref[...], w13_ref[:, ff + c : ff + c + COLS], 1, 0)
+        dh = dot(dy_ref[...], w2_ref[c : c + COLS, :], 1, 1)
         sig = jax.nn.sigmoid(gate)
         act = gate * sig
-        h_ref[sl, :] = (act * up).astype(jnp.bfloat16)
-        z_ref[sl, :ff] = (dh * up * (sig + act * (1.0 - sig))).astype(jnp.bfloat16)
-        z_ref[sl, ff:] = (dh * act).astype(jnp.bfloat16)
-        put_dx(r, dot(z_ref[sl, :], w13[...], 1, 1))
+        h_ref[:, c : c + COLS] = (act * up).astype(jnp.bfloat16)
+        z_ref[:, c : c + COLS] = (dh * up * (sig + act * (1.0 - sig))).astype(jnp.bfloat16)
+        z_ref[:, ff + c : ff + c + COLS] = (dh * act).astype(jnp.bfloat16)
     dw13 = dot(x_ref[...], z_ref[...], 0, 0)
-    terms = (dw13[:, :ff], dw13[:, ff:], dot(dy_ref[...], h_ref[...], 0, 0))
-    for slab, term in enumerate(terms):
-        dw_ref[slab] = jnp.where(first, 0.0, dw_ref[slab]) + term
+    for slab in range(2):
+        dw_ref[slab] = jnp.where(first, 0.0, dw_ref[slab]) + dw13[:, slab * ff : (slab + 1) * ff]
+    dw_ref[2] = jnp.where(first, 0.0, dw_ref[2]) + dot(dy_ref[...], h_ref[...], 0, 0)
+    put_dx(dot(z_ref[...], w13_ref[...], 1, 1))
 
 
 def first_kernel(
     x_ref, dy_ref, g_ref, w1_ref, w3_ref, w2_ref,
     dxp_ref, dws_ref, f1_ref, f3_ref, f2_ref, r_ref, c_ref,
-    acc_ref, w13s_ref, w2s_ref, z_ref, h_ref, send_ref, own_ref, core_ref, row_ref,
+    acc_ref, w13_ref, w2c_ref, w13s_ref, w2s_ref, z_ref, h_ref, send_ref, own_ref, core_ref, row_ref,
     w_loc, w_core, w_row, w_fwd, a_sem, b_sem, c_sem, out_sem, dx_sem,
 ):
     shard, tile = pl.program_id(0), pl.program_id(1)
@@ -70,14 +77,17 @@
             src_ref=src, dst_ref=dst, send_sem=sems.at[0, k], recv_sem=sems.at[1, k], device_id=to, device_id_type=MESH
         )
 
-    def slots(s):
-        return w13s_ref.at[s, :, :ff], w13s_ref.at[s, :, ff:], w2s_ref.at[s]
+    def slots(w13, w2):
+        return w13.at[:, :ff], w13.at[:, ff:], w2
+
+    now = slots(w13_ref, w2c_ref)
+    near, far = (slots(w13s_ref.at[s], w2s_ref.at[s]) for s in range(2))
 
     weights = (w1_ref, w3_ref, w2_ref)
-    local = [pltpu.make_async_copy(w, d, w_loc.at[k]) for k, (w, d) in enumerate(zip(weights, slots(0)))]
-    to_mate = [push(w, d, w_core, k, mate) for k, (w, d) in enumerate(zip(weights, slots(1)))]
-    to_row = [push(w, d, w_row, k, across) for k, (w, d) in enumerate(zip(weights, slots(2)))]
-    forward = [push(w, d, w_fwd, k, mate) for k, (w, d) in enumerate(zip(slots(2), (f1_ref, f3_ref, f2_ref)))]
+    local = [pltpu.make_async_copy(w, d, w_loc.at[k]) for k, (w, d) in enumerate(zip(weights, now))]
+    to_mate = [push(w, d, w_core, k, mate) for k, (w, d) in enumerate(zip(weights, near))]
+    to_row = [push(w, d, w_row, k, across) for k, (w, d) in enumerate(zip(weights, far))]
+    forward = [push(w, d, w_fwd, k, mate) for k, (w, d) in enumerate(zip(far, (f1_ref, f3_ref, f2_ref)))]
 
     def rows_of(c):
         return pl.ds(pl.multiple_of(c * chunk, 16), chunk)
@@ -98,6 +108,19 @@
 
     def dx_out(t):
         return pltpu.make_async_copy(acc_ref.at[dx_rows(t), :], dxp_ref.at[dx_rows(t), :], dx_sem.at[t])
+
+    def take(s):
+        def rows13(sl):
+            w13_ref[sl, :] = w13s_ref[s, sl, :]
+
+        def rows2(sl):
+            w2c_ref[sl, :] = w2s_ref[s, sl, :]
+
+        by_rows(w13_ref.shape[0], 64, rows13)
+        by_rows(ff, 64, rows2)
+
+    def at(c, sl):
+        return pl.ds(pl.multiple_of(c * chunk + sl.start, 16), sl.size)
 
     @pl.when(step == 0)
     def _():
@@ -116,6 +139,11 @@
     def _():
         for copy in to_mate:
             copy.wait_recv()
+        take(0)
+
+    @pl.when(step == 2 * tiles)
+    def _():
+        take(1)
 
     @pl.when(step == FORWARD)
     def _():
@@ -134,11 +162,14 @@
         def _():
             core_push(step - 2).wait_send()
 
-        for k, r in enumerate((row, 1 - row)):
-            mine = pl.ds(pl.multiple_of((2 * r + core) * ff, ff), ff)
-            theirs = pl.ds(pl.multiple_of((2 * r + 1 - core) * ff, ff), ff)
-            own_ref[k, rows_of(step), :] = g_ref[:, mine].astype(jnp.bfloat16)
-            send_ref[lax.rem(step, 2), k] = g_ref[:, theirs].astype(jnp.bfloat16)
+        def convert(sl):
+            for k, r in enumerate((row, 1 - row)):
+                mine = pl.ds(pl.multiple_of((2 * r + core) * ff, ff), ff)
+                theirs = pl.ds(pl.multiple_of((2 * r + 1 - core) * ff, ff), ff)
+                own_ref[k, at(step, sl), :] = g_ref[sl, mine].astype(jnp.bfloat16)
+                send_ref[lax.rem(step, 2), k, sl, :] = g_ref[sl, theirs].astype(jnp.bfloat16)
+
+        by_rows(chunk, 16, convert)
 
     @pl.when((step > CORE_SUM) & (step <= CORE_SUM + CHUNKS))
     def _():
@@ -148,8 +179,12 @@
     def _():
         c = step - CORE_SUM
         core_push(c).wait_recv()
-        for k in range(2):
-            own_ref[k, rows_of(c), :] = wide_sum(own_ref[k, rows_of(c), :], core_ref[k, rows_of(c), :])
+
+        def add(sl):
+            for k in range(2):
+                own_ref[k, at(c, sl), :] = wide_sum(own_ref[k, at(c, sl), :], core_ref[k, at(c, sl), :])
+
+        by_rows(chunk, 16, add)
 
     @pl.when((step > ROW_SUM) & (step <= ROW_SUM + CHUNKS // 2))
     def _():
@@ -159,9 +194,13 @@
     @pl.when((step >= ROW_SUM) & (step < ROW_SUM + CHUNKS // 2))
     def _():
         for k in range(2):
-            c = 2 * (step - ROW_SUM) + k
-            row_push(c).wait_recv()
-            own_ref[0, rows_of(c), :] = wide_sum(own_ref[0, rows_of(c), :], row_ref[rows_of(c), :])
+            row_push(2 * (step - ROW_SUM) + k).wait_recv()
+
+        def add(sl):
+            sl = at(2 * (step - ROW_SUM), sl)
+            own_ref[0, sl, :] = wide_sum(own_ref[0, sl, :], row_ref[sl, :])
+
+        by_rows(2 * chunk, 32, add)
 
     @pl.when(step == ROW_SUM + CHUNKS // 2 + 1)
     def _():
@@ -171,13 +210,10 @@
     def _():
         dx_out(tile - 1).start()
 
-    rows = TILE1 // 2
-
-    def put_dx(r, dx):
-        sl = pl.ds(pl.multiple_of(tile * TILE1 + r * rows, rows), rows)
-        acc_ref[sl, :] = jnp.where(shard == 0, 0.0, acc_ref[sl, :]) + dx
-
-    backward_tile(x_ref, dy_ref, w13s_ref.at[shard], w2s_ref.at[shard], z_ref, h_ref, dws_ref.at[0], tile == 0, rows, put_dx)
+    def put_dx(dx):
+        acc_ref[dx_rows(tile), :] = jnp.where(shard == 0, 0.0, acc_ref[dx_rows(tile), :]) + dx
+
+    backward_tile(x_ref, dy_ref, w13_ref, w2c_ref, z_ref, h_ref, dws_ref.at[0], tile == 0, put_dx)
 
     @pl.when(step == steps - 1)
     def _():
@@ -220,8 +256,10 @@
         ],
         scratch_shapes=[
             pltpu.VMEM((tokens, d), f32),
-            pltpu.VMEM((SHARDS1, d, 2 * ff), bf16),
-            pltpu.VMEM((SHARDS1, ff, d), bf16),
+            pltpu.VMEM((d, 2 * ff), bf16),
+            pltpu.VMEM((ff, d), bf16),
+            pltpu.VMEM((SHARDS1 - 1, d, 2 * ff), bf16),
+            pltpu.VMEM((SHARDS1 - 1, ff, d), bf16),
             pltpu.VMEM((TILE1, 2 * ff), bf16),
             pltpu.VMEM((TILE1, ff), bf16),
             pltpu.VMEM((2, 2, chunk, ff), bf16),
@@ -249,34 +287,53 @@
 def last_kernel(
     x_ref, dy_ref, dxp_ref, dws_ref, w1_ref, w3_ref, w2_ref, r_ref, c_ref,
     dx_ref, next_ref, dw_ref,
-    w13s_ref, z_ref, h_ref, dw_acc, move_sem, own_sem,
+    w13s_ref, z_ref, h_ref, dw_acc, move_ref, in_sem, move_sem, own_sem,
 ):
     tile, tiles = pl.program_id(0), pl.num_programs(0)
     row, core = lax.axis_index("row"), lax.axis_index("fsdp")
     ff = h_ref.shape[1]
-    block = dws_ref.shape[2]
     cols = [2 * row + core, 2 * row + 1 - core, 2 * (1 - row) + core, 2 * (1 - row) + 1 - core]
     lanes = [pl.ds(pl.multiple_of(q * ff, ff), ff) for q in cols]
-    span = pl.ds(pl.multiple_of(tile * block, block), block)
-    moves = [pltpu.make_async_copy(dws_ref.at[s], dw_ref.at[:, span, lanes[s]], move_sem.at[s]) for s in range(SHARDS1)]
-    for move in moves:
-        move.start()
+    moves = dws_ref.shape[2] // MOVE
+
+    def span(m):
+        return pl.ds(pl.multiple_of(m * MOVE, MOVE), MOVE)
+
+    def fetch(m):
+        return pltpu.make_async_copy(dws_ref.at[:, :, span(m), :], move_ref.at[lax.rem(m, 2)], in_sem.at[lax.rem(m, 2)])
+
+    def place(m):
+        return [pltpu.make_async_copy(move_ref.at[lax.rem(m, 2), s], dw_ref.at[:, span(m), lanes[s]], move_sem.at[lax.rem(m, 2), s]) for s in range(SHARDS1)]
+
+    @pl.when((tile >= 2) & (tile < moves + 2))
+    def _():
+        for copy in place(tile - 2):
+            copy.wait()
+
+    @pl.when(tile < moves)
+    def _():
+        fetch(tile).start()
+
+    @pl.when((tile >= 1) & (tile < moves + 1))
+    def _():
+        fetch(tile - 1).wait()
+        for copy in place(tile - 1):
+            copy.start()
 
     @pl.when(tile == 0)
     def _():
-        w13s_ref[:, :ff] = w1_ref[...]
-        w13s_ref[:, ff:] = w3_ref[...]
+        def join(sl):
+            w13s_ref[sl, :ff] = w1_ref[sl, :]
+            w13s_ref[sl, ff:] = w3_ref[sl, :]
+
+        by_rows(w1_ref.shape[0], 64, join)
 
     next_ref[...] = r_ref[...].astype(jnp.float32) + c_ref[...].astype(jnp.float32)
-    rows = TILE2 // 2
-
-    def put_dx(r, dx):
-        sl = slice(r * rows, (r + 1) * rows)
-        dx_ref[sl, :] = (dxp_ref[sl, :] + dx).astype(jnp.bfloat16)
-
-    backward_tile(x_ref, dy_ref, w13s_ref, w2_ref, z_ref, h_ref, dw_acc, tile == 0, rows, put_dx)
-    for move in moves:
-        move.wait()
+
+    def put_dx(dx):
+        dx_ref[...] = (dxp_ref[...] + dx).astype(jnp.bfloat16)
+
+    backward_tile(x_ref, dy_ref, w13s_ref, w2_ref, z_ref, h_ref, dw_acc, tile == 0, put_dx)
 
     @pl.when(tile == tiles - 1)
     def _():
@@ -296,7 +353,7 @@
     return pl.pallas_call(
         last_kernel,
         grid=(tiles,),
-        in_specs=[tok, tok, tok, pl.BlockSpec((SHARDS1, 3, d // tiles, ff), lambda j: (0, 0, j, 0)), *[full(w) for w in weights], part, part],
+        in_specs=[tok, tok, tok, pl.BlockSpec(memory_space=pltpu.HBM), *[full(w) for w in weights], part, part],
         out_specs=[tok, part, pl.BlockSpec(memory_space=pltpu.HBM)],
         out_shape=[
             jax.ShapeDtypeStruct((tokens, d), jnp.bfloat16),
@@ -308,7 +365,9 @@
             pltpu.VMEM((TILE2, 2 * ff), jnp.bfloat16),
             pltpu.VMEM((TILE2, ff), jnp.bfloat16),
             pltpu.VMEM((3, d, ff), jnp.float32),
-            pltpu.SemaphoreType.DMA((SHARDS1,)),
+            pltpu.VMEM((2, SHARDS1, 3, MOVE, ff), jnp.float32),
+            pltpu.SemaphoreType.DMA((2,)),
+            pltpu.SemaphoreType.DMA((2, SHARDS1)),
             pltpu.SemaphoreType.DMA(()),
         ],
         compiler_params=pltpu.CompilerParams(vmem_limit_bytes=VMEM_BYTES, dimension_semantics=("arbitrary",)),

time: 202 us -> 196 us (0.970)
  Pallas kernels: 201 us -> 195 us
    pallas_call x1, Pallas kernels: 52.9 us -> 48.9 us  [run_last(): pl.pallas_call(last_kernel, grid=(tiles,), in_specs=[tok, tok, tok, pl.Bl...]
    pallas_call x1, Pallas kernels: 148 us -> 146 us  [run_first(): pl.pallas_call(first_kernel, grid=(SHARDS1, tiles), in_specs=[tok, tok, p...]
where the time goes in v2:
time: 196 us; the launch traced here: 195 us
  Pallas kernels  195 us (99%)
    pallas_call x1, Pallas kernels, run_first(): pl.pallas_call(first_kernel, grid=(SHARDS1, tiles), in_specs=[tok, tok, p...  146 us
    pallas_call x1, Pallas kernels, run_last(): pl.pallas_call(last_kernel, grid=(tiles,), in_specs=[tok, tok, tok, pl.Bl...  48.9 us

profile of v2, /device:TPU:0, one launch (start us, length us, event | category | flops | bytes accessed | tf_op | source)
XLA Modules:
  0.0 195.4 jit_solution(3002360636998250104)
XLA Ops:
  0.6 145.9 %bwd_first.1 = (f32[6144,768]{1,0:T(8,128)}, f32[3,3,768,512]{3,2,1,0:T(8,128)}, bf16[768,512]{1,0:T(8,128)(2,1)}, bf16[768,512]{1,0:T(8,128)(2,1)}, bf16[512,76...) custom-call(bf16[6144,768]{1,0:T(8,128)(2,1)} %bitcast.7, bf16[6144,768]{1,0:T(8,128)(2,1)} %bitcast.9, ...), custom_call_target="tpu_custom_call" | custom-call | flops 115964116992 | bytes 120000000 | tf_op jit(solution)/shard_map/bwd_first/pallas_call | solution.py:245
  146.5 48.9 %bwd_last.1 = (bf16[6144,768]{1,0:T(8,128)(2,1)}, f32[2304,512]{1,0:T(8,128)}, f32[3,768,2048]{2,1,0:T(8,128)}) custom-call(bf16[6144,768]{1,0:T(8,128)(2,1)} %bitcast.8, bf16[6144,768]{1,0:T(8,128)(2,1)} %bitcast.10, f32[6144,768]{1,0:T(8,128)} %get-tuple-element.13.dxp_ref, f32[3,3,768,512]{3,2,1,0:T(8,128)} %get-tuple-element.14.dws_ref, ...), custom_call_target="tpu_custom_call" | custom-call | flops 38654705664 | bytes 90000000 | tf_op jit(solution)/shard_map/bwd_last/pallas_call | solution.py:353

commit v3 on v2

--- a/solution.py
+++ b/solution.py
@@ -18,17 +18,18 @@
 MOVE = 128
 SHARDS1 = 3
 CHUNKS = 16
-CORE_SUM = 3
-ROW_SUM = 14
-FORWARD = 12
+SPREAD = 6
+CORE_SUM = 2
+ROW_SUM = 6
+FORWARD = 14
 
 
 def dot(lhs, rhs, lhs_dim, rhs_dim):
     return lax.dot_general(lhs, rhs, (((lhs_dim,), (rhs_dim,)), ((), ())), preferred_element_type=jnp.float32)
 
 
-def wide_sum(a, b):
-    return (a.astype(jnp.float32) + b.astype(jnp.float32)).astype(jnp.bfloat16)
+def seldom(cond):
+    return pl.loop(0, cond.astype(jnp.int32))
 
 
 def by_rows(rows, block, body):
@@ -37,7 +38,7 @@
         body(pl.ds(pl.multiple_of(i * block, block), block))
 
 
-def backward_tile(x_ref, dy_ref, w13_ref, w2_ref, z_ref, h_ref, dw_ref, first, put_dx):
+def backward_tile(x_ref, dy_ref, w13_ref, w2_ref, z_ref, h_ref, dw_ref, first, put_dx, before=(None,)):
     ff = h_ref.shape[1]
     for c in range(0, ff, COLS):
         gate = dot(x_ref[...], w13_ref[:, c : c + COLS], 1, 0)
@@ -52,14 +53,18 @@
     for slab in range(2):
         dw_ref[slab] = jnp.where(first, 0.0, dw_ref[slab]) + dw13[:, slab * ff : (slab + 1) * ff]
     dw_ref[2] = jnp.where(first, 0.0, dw_ref[2]) + dot(dy_ref[...], h_ref[...], 0, 0)
-    put_dx(dot(z_ref[...], w13_ref[...], 1, 1))
+    rows = z_ref.shape[0] // len(before)
+    for k, call in enumerate(before):
+        if call is not None:
+            call()
+        put_dx(k * rows, rows, dot(z_ref[k * rows : (k + 1) * rows, :], w13_ref[...], 1, 1))
 
 
 def first_kernel(
     x_ref, dy_ref, g_ref, w1_ref, w3_ref, w2_ref,
     dxp_ref, dws_ref, f1_ref, f3_ref, f2_ref, r_ref, c_ref,
-    acc_ref, w13_ref, w2c_ref, w13s_ref, w2s_ref, z_ref, h_ref, send_ref, own_ref, core_ref, row_ref,
-    w_loc, w_core, w_row, w_fwd, a_sem, b_sem, c_sem, out_sem, dx_sem,
+    acc_ref, dw_ref, w13_ref, w2c_ref, w13s_ref, w2s_ref, z_ref, h_ref, send_ref, own_ref, core_ref, row_ref,
+    w_loc, w_core, w_row, w_rep, w_fwd, a_sem, b_sem, c_sem, out_sem, dx_sem, dw_sem,
 ):
     shard, tile = pl.program_id(0), pl.program_id(1)
     tiles = pl.num_programs(1)
@@ -86,8 +91,14 @@
     weights = (w1_ref, w3_ref, w2_ref)
     local = [pltpu.make_async_copy(w, d, w_loc.at[k]) for k, (w, d) in enumerate(zip(weights, now))]
     to_mate = [push(w, d, w_core, k, mate) for k, (w, d) in enumerate(zip(weights, near))]
-    to_row = [push(w, d, w_row, k, across) for k, (w, d) in enumerate(zip(weights, far))]
     forward = [push(w, d, w_fwd, k, mate) for k, (w, d) in enumerate(zip(far, (f1_ref, f3_ref, f2_ref)))]
+
+    def half(v):
+        rows = v.shape[0] // 2
+        return v.at[pl.ds(pl.multiple_of(dp * rows, 16), rows), :]
+
+    to_row = [push(half(w), half(d), w_row, k, across) for k, (w, d) in enumerate(zip(weights, far))]
+    spread = [push(half(d), half(d), w_rep, k, replica) for k, d in enumerate(far)]
 
     def rows_of(c):
         return pl.ds(pl.multiple_of(c * chunk, 16), chunk)
@@ -103,11 +114,14 @@
 
     keep_sum = pltpu.make_async_copy(own_ref.at[0], r_ref, out_sem)
 
-    def dx_rows(t):
-        return pl.ds(pl.multiple_of(t * TILE1, TILE1), TILE1)
-
-    def dx_out(t):
-        return pltpu.make_async_copy(acc_ref.at[dx_rows(t), :], dxp_ref.at[dx_rows(t), :], dx_sem.at[t])
+    def dx_out(start, rows, k):
+        sl = pl.ds(pl.multiple_of(start, 16), rows)
+        return pltpu.make_async_copy(acc_ref.at[sl, :], dxp_ref.at[sl, :], dx_sem.at[k])
+
+    third = TILE1 // 3
+    dx_outs = [dx_out(t * TILE1, TILE1, t) for t in range(acc_ref.shape[0] // TILE1 - 1)]
+    dx_lasts = [dx_out(acc_ref.shape[0] - TILE1 + k * third, third, len(dx_outs) + k) for k in range(3)]
+    dw_outs = [pltpu.make_async_copy(dw_ref.at[k % 2], dws_ref.at[k], dw_sem.at[k]) for k in range(SHARDS1)]
 
     def take(s):
         def rows13(sl):
@@ -116,41 +130,59 @@
         def rows2(sl):
             w2c_ref[sl, :] = w2s_ref[s, sl, :]
 
-        by_rows(w13_ref.shape[0], 64, rows13)
-        by_rows(ff, 64, rows2)
+        by_rows(w13_ref.shape[0], 128, rows13)
+        by_rows(ff, 128, rows2)
 
     def at(c, sl):
         return pl.ds(pl.multiple_of(c * chunk + sl.start, 16), sl.size)
 
-    @pl.when(step == 0)
-    def _():
-        barrier = pltpu.get_barrier_semaphore()
-        for to in (mate, across, replica):
-            pl.semaphore_signal(barrier, inc=1, device_id=to, device_id_type=MESH)
-        for copy in local:
-            copy.start()
-        pl.semaphore_wait(barrier, 3)
-        for copy in (*to_row, *to_mate):
-            copy.start()
-        for copy in local:
-            copy.wait()
-
-    @pl.when(step == tiles)
-    def _():
-        for copy in to_mate:
-            copy.wait_recv()
-        take(0)
-
-    @pl.when(step == 2 * tiles)
-    def _():
-        take(1)
-
-    @pl.when(step == FORWARD)
-    def _():
-        for copy in to_row:
-            copy.wait_recv()
-        for copy in forward:
-            copy.start()
+    turns = (0, SPREAD, tiles, FORWARD, 2 * tiles, ROW_SUM + CHUNKS + 1)
+
+    @seldom(functools.reduce(jnp.logical_or, [step == t for t in turns]))
+    def _(_):
+        @pl.when(step == 0)
+        def _():
+            barrier = pltpu.get_barrier_semaphore()
+            for to in (mate, across, replica):
+                pl.semaphore_signal(barrier, inc=1, device_id=to, device_id_type=MESH)
+            for copy in local:
+                copy.start()
+            pl.semaphore_wait(barrier, 3)
+            for copy in (*to_row, *to_mate):
+                copy.start()
+            for copy in local:
+                copy.wait()
+
+        @pl.when(step == tiles)
+        def _():
+            for copy in to_mate:
+                copy.wait_recv()
+            take(0)
+            dw_outs[0].start()
+
+        @pl.when(step == 2 * tiles)
+        def _():
+            take(1)
+            dw_outs[1].start()
+            dw_outs[0].wait()
+
+        @pl.when(step == SPREAD)
+        def _():
+            for copy in to_row:
+                copy.wait_recv()
+            for copy in spread:
+                copy.start()
+
+        @pl.when(step == FORWARD)
+        def _():
+            for copy in spread:
+                copy.wait_recv()
+            for copy in forward:
+                copy.start()
+
+        @pl.when(step == ROW_SUM + CHUNKS + 1)
+        def _():
+            keep_sum.start()
 
     @pl.when((step >= 1) & (step <= CHUNKS))
     def _():
@@ -169,7 +201,7 @@
                 own_ref[k, at(step, sl), :] = g_ref[sl, mine].astype(jnp.bfloat16)
                 send_ref[lax.rem(step, 2), k, sl, :] = g_ref[sl, theirs].astype(jnp.bfloat16)
 
-        by_rows(chunk, 16, convert)
+        by_rows(chunk, 48, convert)
 
     @pl.when((step > CORE_SUM) & (step <= CORE_SUM + CHUNKS))
     def _():
@@ -182,43 +214,45 @@
 
         def add(sl):
             for k in range(2):
-                own_ref[k, at(c, sl), :] = wide_sum(own_ref[k, at(c, sl), :], core_ref[k, at(c, sl), :])
-
-        by_rows(chunk, 16, add)
-
-    @pl.when((step > ROW_SUM) & (step <= ROW_SUM + CHUNKS // 2))
-    def _():
-        for k in range(2):
-            dp_push(2 * (step - ROW_SUM - 1) + k).start()
-
-    @pl.when((step >= ROW_SUM) & (step < ROW_SUM + CHUNKS // 2))
-    def _():
-        for k in range(2):
-            row_push(2 * (step - ROW_SUM) + k).wait_recv()
+                own_ref[k, at(c, sl), :] = own_ref[k, at(c, sl), :] + core_ref[k, at(c, sl), :]
+
+        by_rows(chunk, 48, add)
+
+    @pl.when((step > ROW_SUM) & (step <= ROW_SUM + CHUNKS))
+    def _():
+        dp_push(step - ROW_SUM - 1).start()
+
+    @pl.when((step >= ROW_SUM) & (step < ROW_SUM + CHUNKS))
+    def _():
+        c = step - ROW_SUM
+        row_push(c).wait_recv()
 
         def add(sl):
-            sl = at(2 * (step - ROW_SUM), sl)
-            own_ref[0, sl, :] = wide_sum(own_ref[0, sl, :], row_ref[sl, :])
-
-        by_rows(2 * chunk, 32, add)
-
-    @pl.when(step == ROW_SUM + CHUNKS // 2 + 1)
-    def _():
-        keep_sum.start()
+            own_ref[0, at(c, sl), :] = own_ref[0, at(c, sl), :] + row_ref[at(c, sl), :]
+
+        by_rows(chunk, 48, add)
 
     @pl.when(step > steps - tiles)
     def _():
-        dx_out(tile - 1).start()
-
-    def put_dx(dx):
-        acc_ref[dx_rows(tile), :] = jnp.where(shard == 0, 0.0, acc_ref[dx_rows(tile), :]) + dx
-
-    backward_tile(x_ref, dy_ref, w13_ref, w2c_ref, z_ref, h_ref, dws_ref.at[0], tile == 0, put_dx)
-
-    @pl.when(step == steps - 1)
-    def _():
-        dx_out(tile).start()
-        for copy in (*to_mate, *to_row):
+        dx_out((tile - 1) * TILE1, TILE1, tile - 1).start()
+
+    def put_dx(start, rows, dx):
+        sl = pl.ds(pl.multiple_of(tile * TILE1 + start, 16), rows)
+        acc_ref[sl, :] = jnp.where(shard == 0, 0.0, acc_ref[sl, :]) + dx
+
+    def compute(**extra):
+        backward_tile(x_ref, dy_ref, w13_ref, w2c_ref, z_ref, h_ref, dw_ref.at[lax.rem(shard, 2)], tile == 0, put_dx, **extra)
+
+    @pl.when(step < steps - 1)
+    def _():
+        compute()
+
+    @seldom(step == steps - 1)
+    def _(_):
+        compute(before=(None, dw_outs[2].start, dx_lasts[0].start))
+        for copy in dx_lasts[1:]:
+            copy.start()
+        for copy in (*to_mate, *to_row, *spread):
             copy.wait_send()
         for copy in forward:
             copy.wait()
@@ -228,8 +262,8 @@
             row_push(c).wait_send()
             dp_push(c).wait()
         keep_sum.wait()
-        for t in range(dxp_ref.shape[0] // TILE1):
-            dx_out(t).wait()
+        for copy in (*dw_outs[1:], *dx_outs, *dx_lasts):
+            copy.wait()
 
 
 def run_first(x, dy, weights, g):
@@ -246,7 +280,7 @@
         first_kernel,
         grid=(SHARDS1, tiles),
         in_specs=[tok, tok, pl.BlockSpec((chunk, g_cols), lambda s, j: (jnp.minimum(s * tiles + j, CHUNKS - 1), 0)), hbm, hbm, hbm],
-        out_specs=[hbm, pl.BlockSpec((1, 3, d, ff), lambda s, j: (s, 0, 0, 0)), hbm, hbm, hbm, hbm, hbm],
+        out_specs=[hbm, hbm, hbm, hbm, hbm, hbm, hbm],
         out_shape=[
             jax.ShapeDtypeStruct((tokens, d), f32),
             jax.ShapeDtypeStruct((SHARDS1, 3, d, ff), f32),
@@ -256,6 +290,7 @@
         ],
         scratch_shapes=[
             pltpu.VMEM((tokens, d), f32),
+            pltpu.VMEM((2, 3, d, ff), f32),
             pltpu.VMEM((d, 2 * ff), bf16),
             pltpu.VMEM((ff, d), bf16),
             pltpu.VMEM((SHARDS1 - 1, d, 2 * ff), bf16),
@@ -270,11 +305,13 @@
             dma((2, 3)),
             dma((2, 3)),
             dma((2, 3)),
+            dma((2, 3)),
             dma((2, CHUNKS)),
             dma((2, CHUNKS)),
             dma((2, CHUNKS)),
             dma(()),
-            dma((tiles,)),
+            dma((tiles + 2,)),
+            dma((SHARDS1,)),
         ],
         compiler_params=pltpu.CompilerParams(
             vmem_limit_bytes=VMEM_BYTES, dimension_semantics=("arbitrary", "arbitrary"), collective_id=0, has_side_effects=True
@@ -326,19 +363,25 @@
             w13s_ref[sl, :ff] = w1_ref[sl, :]
             w13s_ref[sl, ff:] = w3_ref[sl, :]
 
-        by_rows(w1_ref.shape[0], 64, join)
+        by_rows(w1_ref.shape[0], 256, join)
 
     next_ref[...] = r_ref[...].astype(jnp.float32) + c_ref[...].astype(jnp.float32)
 
-    def put_dx(dx):
-        dx_ref[...] = (dxp_ref[...] + dx).astype(jnp.bfloat16)
-
-    backward_tile(x_ref, dy_ref, w13s_ref, w2_ref, z_ref, h_ref, dw_acc, tile == 0, put_dx)
+    def put_dx(start, rows, dx):
+        sl = slice(start, start + rows)
+        dx_ref[sl, :] = (dxp_ref[sl, :] + dx).astype(jnp.bfloat16)
+
+    def compute(**extra):
+        backward_tile(x_ref, dy_ref, w13s_ref, w2_ref, z_ref, h_ref, dw_acc, tile == 0, put_dx, **extra)
+
+    @pl.when(tile < tiles - 1)
+    def _():
+        compute()
 
     @pl.when(tile == tiles - 1)
     def _():
         own = pltpu.make_async_copy(dw_acc, dw_ref.at[:, :, lanes[3]], own_sem)
-        own.start()
+        compute(before=(None, own.start))
         own.wait()
 
 

time: 196 us -> 187 us (0.954)
  Pallas kernels: 195 us -> 186 us
    pallas_call x1, Pallas kernels: 146 us -> 137 us  [run_first(): pl.pallas_call(first_kernel, grid=(SHARDS1, tiles), in_specs=[tok, tok, p...]
where the time goes in v3:
time: 187 us
  Pallas kernels  186 us (99%)
    pallas_call x1, Pallas kernels, run_first(): pl.pallas_call(first_kernel, grid=(SHARDS1, tiles), in_specs=[tok, tok, p...  137 us
    pallas_call x1, Pallas kernels, run_last(): pl.pallas_call(last_kernel, grid=(tiles,), in_specs=[tok, tok, tok, pl.Bl...  48.8 us

profile of v3, /device:TPU:0, one launch (start us, length us, event | category | flops | bytes accessed | tf_op | source)
XLA Modules:
  0.0 186.9 jit_solution(17517820180406200388)
XLA Ops:
  0.6 137.4 %bwd_first.1 = (f32[6144,768]{1,0:T(8,128)}, f32[3,3,768,512]{3,2,1,0:T(8,128)}, bf16[768,512]{1,0:T(8,128)(2,1)}, bf16[768,512]{1,0:T(8,128)(2,1)}, bf16[512,76...) custom-call(bf16[6144,768]{1,0:T(8,128)(2,1)} %bitcast.7, bf16[6144,768]{1,0:T(8,128)(2,1)} %bitcast.9, ...), custom_call_target="tpu_custom_call" | custom-call | flops 115964116992 | bytes 120000000 | tf_op jit(solution)/shard_map/bwd_first/pallas_call | solution.py:279
  138.0 48.8 %bwd_last.1 = (bf16[6144,768]{1,0:T(8,128)(2,1)}, f32[2304,512]{1,0:T(8,128)}, f32[3,768,2048]{2,1,0:T(8,128)}) custom-call(bf16[6144,768]{1,0:T(8,128)(2,1)} %bitcast.8, bf16[6144,768]{1,0:T(8,128)(2,1)} %bitcast.10, f32[6144,768]{1,0:T(8,128)} %get-tuple-element.13.dxp_ref, f32[3,3,768,512]{3,2,1,0:T(8,128)} %get-tuple-element.14.dws_ref, ...), custom_call_target="tpu_custom_call" | custom-call | flops 38654705664 | bytes 90000000 | tf_op jit(solution)/shard_map/bwd_last/pallas_call | solution.py:396

commit v4 on v3

--- a/solution.py
+++ b/solution.py
@@ -18,9 +18,9 @@
 MOVE = 128
 SHARDS1 = 3
 CHUNKS = 16
-SPREAD = 6
+SPREAD = 7
 CORE_SUM = 2
-ROW_SUM = 6
+ROW_SUM = 7
 FORWARD = 14
 
 
@@ -38,7 +38,7 @@
         body(pl.ds(pl.multiple_of(i * block, block), block))
 
 
-def backward_tile(x_ref, dy_ref, w13_ref, w2_ref, z_ref, h_ref, dw_ref, first, put_dx, before=(None,)):
+def backward_tile(x_ref, dy_ref, w13_ref, w2_ref, z_ref, h_ref, dw_ref, first, put_dx, aside, before=(None,)):
     ff = h_ref.shape[1]
     for c in range(0, ff, COLS):
         gate = dot(x_ref[...], w13_ref[:, c : c + COLS], 1, 0)
@@ -53,6 +53,7 @@
     for slab in range(2):
         dw_ref[slab] = jnp.where(first, 0.0, dw_ref[slab]) + dw13[:, slab * ff : (slab + 1) * ff]
     dw_ref[2] = jnp.where(first, 0.0, dw_ref[2]) + dot(dy_ref[...], h_ref[...], 0, 0)
+    aside()
     rows = z_ref.shape[0] // len(before)
     for k, call in enumerate(before):
         if call is not None:
@@ -112,7 +113,7 @@
     def dp_push(c):
         return push(own_ref.at[0, rows_of(c), :], c_ref.at[rows_of(c), :], c_sem, c, replica)
 
-    keep_sum = pltpu.make_async_copy(own_ref.at[0], r_ref, out_sem)
+    keep_sum = pltpu.make_async_copy(own_ref.at[0, : r_ref.shape[0], :], r_ref, out_sem)
 
     def dx_out(start, rows, k):
         sl = pl.ds(pl.multiple_of(start, 16), rows)
@@ -133,25 +134,26 @@
         by_rows(w13_ref.shape[0], 128, rows13)
         by_rows(ff, 128, rows2)
 
-    def at(c, sl):
-        return pl.ds(pl.multiple_of(c * chunk + sl.start, 16), sl.size)
-
-    turns = (0, SPREAD, tiles, FORWARD, 2 * tiles, ROW_SUM + CHUNKS + 1)
+    turns = (0, 1, SPREAD, tiles, FORWARD, 2 * tiles, ROW_SUM + CHUNKS)
 
     @seldom(functools.reduce(jnp.logical_or, [step == t for t in turns]))
     def _(_):
+        barrier = pltpu.get_barrier_semaphore()
+
         @pl.when(step == 0)
         def _():
-            barrier = pltpu.get_barrier_semaphore()
             for to in (mate, across, replica):
                 pl.semaphore_signal(barrier, inc=1, device_id=to, device_id_type=MESH)
             for copy in local:
                 copy.start()
+            for copy in local:
+                copy.wait()
+
+        @pl.when(step == 1)
+        def _():
             pl.semaphore_wait(barrier, 3)
             for copy in (*to_row, *to_mate):
                 copy.start()
-            for copy in local:
-                copy.wait()
 
         @pl.when(step == tiles)
         def _():
@@ -180,57 +182,50 @@
             for copy in forward:
                 copy.start()
 
-        @pl.when(step == ROW_SUM + CHUNKS + 1)
+        @pl.when(step == ROW_SUM + CHUNKS)
         def _():
             keep_sum.start()
 
-    @pl.when((step >= 1) & (step <= CHUNKS))
+    def chunk_at(lag):
+        c = step - lag
+        return jnp.where((c >= 0) & (c < CHUNKS), c, CHUNKS)
+
+    def has_chunk(lag):
+        return (step >= lag) & (step < lag + CHUNKS)
+
+    @pl.when(has_chunk(1))
     def _():
         core_push(step - 1).start()
 
-    @pl.when(step < CHUNKS)
-    def _():
-        @pl.when(step >= 2)
-        def _():
-            core_push(step - 2).wait_send()
-
-        def convert(sl):
-            for k, r in enumerate((row, 1 - row)):
-                mine = pl.ds(pl.multiple_of((2 * r + core) * ff, ff), ff)
-                theirs = pl.ds(pl.multiple_of((2 * r + 1 - core) * ff, ff), ff)
-                own_ref[k, at(step, sl), :] = g_ref[sl, mine].astype(jnp.bfloat16)
-                send_ref[lax.rem(step, 2), k, sl, :] = g_ref[sl, theirs].astype(jnp.bfloat16)
-
-        by_rows(chunk, 48, convert)
-
-    @pl.when((step > CORE_SUM) & (step <= CORE_SUM + CHUNKS))
+    @pl.when(has_chunk(2))
+    def _():
+        core_push(step - 2).wait_send()
+
+    @pl.when(has_chunk(CORE_SUM + 1))
     def _():
         row_push(step - CORE_SUM - 1).start()
 
-    @pl.when((step >= CORE_SUM) & (step < CORE_SUM + CHUNKS))
-    def _():
-        c = step - CORE_SUM
-        core_push(c).wait_recv()
-
-        def add(sl):
-            for k in range(2):
-                own_ref[k, at(c, sl), :] = own_ref[k, at(c, sl), :] + core_ref[k, at(c, sl), :]
-
-        by_rows(chunk, 48, add)
-
-    @pl.when((step > ROW_SUM) & (step <= ROW_SUM + CHUNKS))
+    @pl.when(has_chunk(CORE_SUM))
+    def _():
+        core_push(step - CORE_SUM).wait_recv()
+
+    @pl.when(has_chunk(ROW_SUM + 1))
     def _():
         dp_push(step - ROW_SUM - 1).start()
 
-    @pl.when((step >= ROW_SUM) & (step < ROW_SUM + CHUNKS))
-    def _():
-        c = step - ROW_SUM
-        row_push(c).wait_recv()
-
-        def add(sl):
-            own_ref[0, at(c, sl), :] = own_ref[0, at(c, sl), :] + row_ref[at(c, sl), :]
-
-        by_rows(chunk, 48, add)
+    @pl.when(has_chunk(ROW_SUM))
+    def _():
+        row_push(step - ROW_SUM).wait_recv()
+
+    def reduce_chunks():
+        now, summed, done = rows_of(chunk_at(0)), rows_of(chunk_at(CORE_SUM)), rows_of(chunk_at(ROW_SUM))
+        own_ref[0, done, :] = own_ref[0, done, :] + row_ref[done, :]
+        own_ref[:, summed, :] = own_ref[:, summed, :] + core_ref[:, summed, :]
+        for k, r in enumerate((row, 1 - row)):
+            mine = pl.ds(pl.multiple_of((2 * r + core) * ff, ff), ff)
+            theirs = pl.ds(pl.multiple_of((2 * r + 1 - core) * ff, ff), ff)
+            own_ref[k, now, :] = g_ref[:, mine].astype(jnp.bfloat16)
+            send_ref[lax.rem(step, 2), k] = g_ref[:, theirs].astype(jnp.bfloat16)
 
     @pl.when(step > steps - tiles)
     def _():
@@ -241,7 +236,7 @@
         acc_ref[sl, :] = jnp.where(shard == 0, 0.0, acc_ref[sl, :]) + dx
 
     def compute(**extra):
-        backward_tile(x_ref, dy_ref, w13_ref, w2c_ref, z_ref, h_ref, dw_ref.at[lax.rem(shard, 2)], tile == 0, put_dx, **extra)
+        backward_tile(x_ref, dy_ref, w13_ref, w2c_ref, z_ref, h_ref, dw_ref.at[lax.rem(shard, 2)], tile == 0, put_dx, reduce_chunks, **extra)
 
     @pl.when(step < steps - 1)
     def _():
@@ -256,8 +251,6 @@
             copy.wait_send()
         for copy in forward:
             copy.wait()
-        core_push(CHUNKS - 2).wait_send()
-        core_push(CHUNKS - 1).wait_send()
         for c in range(CHUNKS):
             row_push(c).wait_send()
             dp_push(c).wait()
@@ -298,9 +291,9 @@
             pltpu.VMEM((TILE1, 2 * ff), bf16),
             pltpu.VMEM((TILE1, ff), bf16),
             pltpu.VMEM((2, 2, chunk, ff), bf16),
-            pltpu.VMEM((2, g_rows, ff), bf16),
-            pltpu.VMEM((2, g_rows, ff), bf16),
-            pltpu.VMEM((g_rows, ff), bf16),
+            pltpu.VMEM((2, g_rows + chunk, ff), bf16),
+            pltpu.VMEM((2, g_rows + chunk, ff), bf16),
+            pltpu.VMEM((g_rows + chunk, ff), bf16),
             dma((3,)),
             dma((2, 3)),
             dma((2, 3)),
@@ -365,14 +358,16 @@
 
         by_rows(w1_ref.shape[0], 256, join)
 
-    next_ref[...] = r_ref[...].astype(jnp.float32) + c_ref[...].astype(jnp.float32)
 
     def put_dx(start, rows, dx):
         sl = slice(start, start + rows)
         dx_ref[sl, :] = (dxp_ref[sl, :] + dx).astype(jnp.bfloat16)
 
+    def add_replicas():
+        next_ref[...] = r_ref[...].astype(jnp.float32) + c_ref[...].astype(jnp.float32)
+
     def compute(**extra):
-        backward_tile(x_ref, dy_ref, w13s_ref, w2_ref, z_ref, h_ref, dw_acc, tile == 0, put_dx, **extra)
+        backward_tile(x_ref, dy_ref, w13s_ref, w2_ref, z_ref, h_ref, dw_acc, tile == 0, put_dx, add_replicas, **extra)
 
     @pl.when(tile < tiles - 1)
     def _():

time: 187 us -> 186 us (level)
  no operation moved by 1% of the time
where the time goes in v4:
time: 186 us
  Pallas kernels  185 us (99%)
    pallas_call x1, Pallas kernels, run_first(): pl.pallas_call(first_kernel, grid=(SHARDS1, tiles), in_specs=[tok, tok, p...  136 us
    pallas_call x1, Pallas kernels, run_last(): pl.pallas_call(last_kernel, grid=(tiles,), in_specs=[tok, tok, tok, pl.Bl...  48.5 us

profile of v4, /device:TPU:0, one launch (start us, length us, event | category | flops | bytes accessed | tf_op | source)
XLA Modules:
  0.0 185.8 jit_solution(8342487755740499507)
XLA Ops:
  0.6 136.5 %bwd_first.1 = (f32[6144,768]{1,0:T(8,128)}, f32[3,3,768,512]{3,2,1,0:T(8,128)}, bf16[768,512]{1,0:T(8,128)(2,1)}, bf16[768,512]{1,0:T(8,128)(2,1)}, bf16[512,76...) custom-call(bf16[6144,768]{1,0:T(8,128)(2,1)} %bitcast.7, bf16[6144,768]{1,0:T(8,128)(2,1)} %bitcast.9, ...), custom_call_target="tpu_custom_call" | custom-call | flops 115964116992 | bytes 120000000 | tf_op jit(solution)/shard_map/bwd_first/pallas_call | solution.py:272
  137.1 48.5 %bwd_last.1 = (bf16[6144,768]{1,0:T(8,128)(2,1)}, f32[2304,512]{1,0:T(8,128)}, f32[3,768,2048]{2,1,0:T(8,128)}) custom-call(bf16[6144,768]{1,0:T(8,128)(2,1)} %bitcast.8, bf16[6144,768]{1,0:T(8,128)(2,1)} %bitcast.10, f32[6144,768]{1,0:T(8,128)} %get-tuple-element.13.dxp_ref, f32[3,3,768,512]{3,2,1,0:T(8,128)} %get-tuple-element.14.dws_ref, ...), custom_call_target="tpu_custom_call" | custom-call | flops 38654705664 | bytes 90000000 | tf_op jit(solution)/shard_map/bwd_last/pallas_call | solution.py:391

commit v5 on v4

--- a/solution.py
+++ b/solution.py
@@ -63,9 +63,9 @@
 
 def first_kernel(
     x_ref, dy_ref, g_ref, w1_ref, w3_ref, w2_ref,
-    dxp_ref, dws_ref, f1_ref, f3_ref, f2_ref, r_ref, c_ref,
+    dxp_ref, dws_ref, f13_ref, f2_ref, r_ref, c_ref,
     acc_ref, dw_ref, w13_ref, w2c_ref, w13s_ref, w2s_ref, z_ref, h_ref, send_ref, own_ref, core_ref, row_ref,
-    w_loc, w_core, w_row, w_rep, w_fwd, a_sem, b_sem, c_sem, out_sem, dx_sem, dw_sem,
+    w_core, w_row, w_rep, w_fwd, a_sem, b_sem, c_sem, out_sem, dx_sem, dw_sem,
 ):
     shard, tile = pl.program_id(0), pl.program_id(1)
     tiles = pl.num_programs(1)
@@ -86,13 +86,11 @@
     def slots(w13, w2):
         return w13.at[:, :ff], w13.at[:, ff:], w2
 
-    now = slots(w13_ref, w2c_ref)
     near, far = (slots(w13s_ref.at[s], w2s_ref.at[s]) for s in range(2))
 
     weights = (w1_ref, w3_ref, w2_ref)
-    local = [pltpu.make_async_copy(w, d, w_loc.at[k]) for k, (w, d) in enumerate(zip(weights, now))]
     to_mate = [push(w, d, w_core, k, mate) for k, (w, d) in enumerate(zip(weights, near))]
-    forward = [push(w, d, w_fwd, k, mate) for k, (w, d) in enumerate(zip(far, (f1_ref, f3_ref, f2_ref)))]
+    forward = [push(w, d, w_fwd, k, mate) for k, (w, d) in enumerate(((w13s_ref.at[1], f13_ref), (w2s_ref.at[1], f2_ref)))]
 
     def half(v):
         rows = v.shape[0] // 2
@@ -144,10 +142,16 @@
         def _():
             for to in (mate, across, replica):
                 pl.semaphore_signal(barrier, inc=1, device_id=to, device_id_type=MESH)
-            for copy in local:
-                copy.start()
-            for copy in local:
-                copy.wait()
+
+            def join(sl):
+                w13_ref[sl, :ff] = w1_ref[sl, :]
+                w13_ref[sl, ff:] = w3_ref[sl, :]
+
+            def keep(sl):
+                w2c_ref[sl, :] = w2_ref[sl, :]
+
+            by_rows(w13_ref.shape[0], 128, join)
+            by_rows(ff, 128, keep)
 
         @pl.when(step == 1)
         def _():
@@ -267,17 +271,18 @@
     tiles = tokens // TILE1
     hbm = pl.BlockSpec(memory_space=pltpu.HBM)
     tok = pl.BlockSpec((TILE1, d), lambda s, j: (j, 0))
+    whole = lambda w: pl.BlockSpec(w.shape, lambda s, j: (0, 0), pipeline_mode=pl.Buffered(1))
     bf16, f32, dma = jnp.bfloat16, jnp.float32, pltpu.SemaphoreType.DMA
-    like = lambda v: jax.ShapeDtypeStruct(v.shape, v.dtype)
     return pl.pallas_call(
         first_kernel,
         grid=(SHARDS1, tiles),
-        in_specs=[tok, tok, pl.BlockSpec((chunk, g_cols), lambda s, j: (jnp.minimum(s * tiles + j, CHUNKS - 1), 0)), hbm, hbm, hbm],
-        out_specs=[hbm, hbm, hbm, hbm, hbm, hbm, hbm],
+        in_specs=[tok, tok, pl.BlockSpec((chunk, g_cols), lambda s, j: (jnp.minimum(s * tiles + j, CHUNKS - 1), 0)), *[whole(w) for w in weights]],
+        out_specs=[hbm] * 6,
         out_shape=[
             jax.ShapeDtypeStruct((tokens, d), f32),
             jax.ShapeDtypeStruct((SHARDS1, 3, d, ff), f32),
-            *[like(w) for w in weights],
+            jax.ShapeDtypeStruct((d, 2 * ff), bf16),
+            jax.ShapeDtypeStruct((ff, d), bf16),
             jax.ShapeDtypeStruct((g_rows, ff), bf16),
             jax.ShapeDtypeStruct((g_rows, ff), bf16),
         ],
@@ -294,7 +299,6 @@
             pltpu.VMEM((2, g_rows + chunk, ff), bf16),
             pltpu.VMEM((2, g_rows + chunk, ff), bf16),
             pltpu.VMEM((g_rows + chunk, ff), bf16),
-            dma((3,)),
             dma((2, 3)),
             dma((2, 3)),
             dma((2, 3)),
@@ -315,13 +319,14 @@
 
 
 def last_kernel(
-    x_ref, dy_ref, dxp_ref, dws_ref, w1_ref, w3_ref, w2_ref, r_ref, c_ref,
+    x_ref, dy_ref, w13_ref, w2_ref, r_ref, c_ref, dxp_ref, dws_ref,
     dx_ref, next_ref, dw_ref,
-    w13s_ref, z_ref, h_ref, dw_acc, move_ref, in_sem, move_sem, own_sem,
+    z_ref, h_ref, dw_acc, move_ref, in_sem, move_sem, own_sem,
 ):
     tile, tiles = pl.program_id(0), pl.num_programs(0)
     row, core = lax.axis_index("row"), lax.axis_index("fsdp")
     ff = h_ref.shape[1]
+
     cols = [2 * row + core, 2 * row + 1 - core, 2 * (1 - row) + core, 2 * (1 - row) + 1 - core]
     lanes = [pl.ds(pl.multiple_of(q * ff, ff), ff) for q in cols]
     moves = dws_ref.shape[2] // MOVE
@@ -350,24 +355,15 @@
         for copy in place(tile - 1):
             copy.start()
 
-    @pl.when(tile == 0)
-    def _():
-        def join(sl):
-            w13s_ref[sl, :ff] = w1_ref[sl, :]
-            w13s_ref[sl, ff:] = w3_ref[sl, :]
-
-        by_rows(w1_ref.shape[0], 256, join)
-
-
     def put_dx(start, rows, dx):
-        sl = slice(start, start + rows)
+        sl = pl.ds(start, rows)
         dx_ref[sl, :] = (dxp_ref[sl, :] + dx).astype(jnp.bfloat16)
 
     def add_replicas():
         next_ref[...] = r_ref[...].astype(jnp.float32) + c_ref[...].astype(jnp.float32)
 
     def compute(**extra):
-        backward_tile(x_ref, dy_ref, w13s_ref, w2_ref, z_ref, h_ref, dw_acc, tile == 0, put_dx, add_replicas, **extra)
+        backward_tile(x_ref, dy_ref, w13_ref, w2_ref, z_ref, h_ref, dw_acc, tile == 0, put_dx, add_replicas, **extra)
 
     @pl.when(tile < tiles - 1)
     def _():
@@ -382,8 +378,9 @@
 
 def run_last(x, dy, dxp, dws, weights, mine, other):
     tokens, d = x.shape
-    ff = weights[0].shape[1]
+    ff = weights[1].shape[0]
     tiles = tokens // TILE2
+    hbm = pl.BlockSpec(memory_space=pltpu.HBM)
     g_rows = mine.shape[0]
     tok = pl.BlockSpec((TILE2, d), lambda j: (j, 0))
     full = lambda w: pl.BlockSpec(w.shape, lambda j: (0, 0))
@@ -391,15 +388,14 @@
     return pl.pallas_call(
         last_kernel,
         grid=(tiles,),
-        in_specs=[tok, tok, tok, pl.BlockSpec(memory_space=pltpu.HBM), *[full(w) for w in weights], part, part],
-        out_specs=[tok, part, pl.BlockSpec(memory_space=pltpu.HBM)],
+        in_specs=[tok, tok, *[full(w) for w in weights], part, part, tok, hbm],
+        out_specs=[tok, part, hbm],
         out_shape=[
             jax.ShapeDtypeStruct((tokens, d), jnp.bfloat16),
             jax.ShapeDtypeStruct((g_rows, ff), jnp.float32),
             jax.ShapeDtypeStruct((3, d, 4 * ff), jnp.float32),
         ],
         scratch_shapes=[
-            pltpu.VMEM((d, 2 * ff), jnp.bfloat16),
             pltpu.VMEM((TILE2, 2 * ff), jnp.bfloat16),
             pltpu.VMEM((TILE2, ff), jnp.bfloat16),
             pltpu.VMEM((3, d, ff), jnp.float32),
@@ -411,7 +407,7 @@
         compiler_params=pltpu.CompilerParams(vmem_limit_bytes=VMEM_BYTES, dimension_semantics=("arbitrary",)),
         cost_estimate=pl.CostEstimate(flops=16 * tokens * d * ff, bytes_accessed=90_000_000, transcendentals=0),
         name="bwd_last",
-    )(x, dy, dxp, dws, *weights, mine, other)
+    )(x, dy, *weights, mine, other, dxp, dws)
 
 
 def solution(mesh):

time: 186 us -> 185 us (level)
  no operation moved by 1% of the time
where the time goes in v5:
time: 185 us
  Pallas kernels  185 us (100%)
    pallas_call x1, Pallas kernels, run_first(): pl.pallas_call(first_kernel, grid=(SHARDS1, tiles), in_specs=[tok, tok, p...  136 us
    pallas_call x1, Pallas kernels, run_last(): pl.pallas_call(last_kernel, grid=(tiles,), in_specs=[tok, tok, *[full(w)...  48.6 us

profile of v5, /device:TPU:0, one launch (start us, length us, event | category | flops | bytes accessed | tf_op | source)
XLA Modules:
  0.0 185.4 jit_solution(8035892075589868282)
XLA Ops:
  0.6 136.0 %bwd_first.1 = (f32[6144,768]{1,0:T(8,128)}, f32[3,3,768,512]{3,2,1,0:T(8,128)}, bf16[768,1024]{1,0:T(8,128)(2,1)}, bf16[512,768]{1,0:T(8,128)(2,1)}, bf16[2304,...) custom-call(bf16[6144,768]{1,0:T(8,128)(2,1)} %bitcast.7, bf16[6144,768]{1,0:T(8,128)(2,1)} %bitcast.9, f32[2304,2048]{1,0:T(8,128)} %bitcast.6, ...), custom_call_target="tpu_custom_call" | custom-call | flops 115964116992 | bytes 120000000 | tf_op jit(solution)/shard_map/bwd_first/pallas_call | solution.py:276
  136.6 48.6 %bwd_last.1 = (bf16[6144,768]{1,0:T(8,128)(2,1)}, f32[2304,512]{1,0:T(8,128)}, f32[3,768,2048]{2,1,0:T(8,128)}) custom-call(bf16[6144,768]{1,0:T(8,128)(2,1)} %bitcast.8, bf16[6144,768]{1,0:T(8,128)(2,1)} %bitcast.10, bf16[768,1024]{1,0:T(8,128)(2,1)} %get-tuple-element.12.w13_ref, bf16[512,768]{1,0:T(8,128)(2,1)} %get-tuple-element.13.w2_ref, ...), custom_call_target="tpu_custom_call" | custom-call | flops 38654705664 | bytes 90000000 | tf_op jit(solution)/shard_map/bwd_last/pallas_call | solution.py:388
